TPU v7x, 32 devices: a whole 2x2x4 slice. The times are simulated.
32 devices in a mesh: aux: 4 (over x, core), ao: 8 (over z, y).
Axes of the slice: x: 2, y: 2, z: 4, core: 2. Of those that a mesh axis runs over, the one named last changes fastest.
Arguments:
- cholesky: bfloat16 [64, 4096, 4096], P('aux', 'ao'), may hold values from -3.5 to 3.5, as said below
- coeffs: bfloat16 [4096, 128], P('ao'), may hold values from -0.09375 to 0.09375
Outputs:
- integrals: float32 [16384, 16384], P('aux', 'ao')
Inputs may be any that keep to these rules, and one draw needn't show every extreme that they name: cholesky[L, mu, nu] = cholesky[L, nu, mu] for every vector L.
All inputs are finite; a program needn't handle non-finite values.
Results may differ from a plain program's by a relative error of at most 0.0091.
Values may be sent and summed in bfloat16 or wider, within the bound.
A program may use at most 192 MiB of HBM per device.

v0:
```python
import functools

import jax
import jax.numpy as jnp
from jax import lax
from jax.experimental import pallas as pl
from jax.experimental.pallas import tpu as pltpu
from jax.sharding import PartitionSpec as P

MESH = pl.DeviceIdType.MESH


def pairs_kernel(
    n_aux, n_ao, depth, group,
    chol, c_ref, left, right,
    basis_c, slabs, part, recv, total, mine,
    slab_sem, c_send, c_recv, p_send, p_recv, r_send, r_recv, l_send, l_recv, own_sem,
):
    a = lax.axis_index("aux")
    o = lax.axis_index("ao")
    nvec, rows, _ = chol.shape
    width = mine.shape[0]
    ratio = n_ao // n_aux
    n_groups = nvec // group

    def slab_copy(v):
        slot = lax.rem(v, depth)
        return pltpu.make_async_copy(chol.at[v], slabs.at[slot], slab_sem.at[slot])

    def first(v, carry):
        slab_copy(v).start()
        return carry

    lax.fori_loop(0, depth, first, 0)

    def rows_of(owner):
        return pl.ds(pl.multiple_of(owner * rows, rows), rows)

    sends = []
    for d in range(1, n_ao):
        copy = pltpu.make_async_remote_copy(
            src_ref=c_ref, dst_ref=basis_c.at[rows_of(o)],
            send_sem=c_send.at[d - 1], recv_sem=c_recv.at[d - 1],
            device_id=(a, lax.rem(o + d, n_ao)), device_id_type=MESH,
        )
        copy.start()
        sends.append(copy)
    basis_c[rows_of(o), :] = c_ref[...]
    for copy in sends:
        copy.wait()

    def part_copy(g, d):
        to = lax.rem(o + d, n_ao)
        these = pl.ds(g * group, group)
        return pltpu.make_async_remote_copy(
            src_ref=part.at[to, these], dst_ref=recv.at[d - 1, these],
            send_sem=p_send.at[g, d - 1], recv_sem=p_recv.at[g, d - 1],
            device_id=(a, to), device_id_type=MESH,
        )

    def one_vector(v, carry):
        slab_copy(v).wait()
        slot = lax.rem(v, depth)
        half = jnp.dot(slabs[slot], basis_c[...], preferred_element_type=jnp.float32)
        value = lax.dot_general(
            c_ref[...], half.astype(jnp.bfloat16), (((0,), (0,)), ((), ())),
            preferred_element_type=jnp.float32,
        )

        @pl.when(v + depth < nvec)
        def _():
            slab_copy(v + depth).start()

        part[:, v] = value.astype(jnp.bfloat16).reshape(n_ao, width, value.shape[1])
        return carry

    def one_group(g, carry):
        lax.fori_loop(g * group, (g + 1) * group, one_vector, 0)
        for d in range(1, n_ao):
            part_copy(g, d).start()
        return carry

    lax.fori_loop(0, n_groups, one_group, 0)

    def finish_group(g, carry):
        for d in range(1, n_ao):
            part_copy(g, d).wait()
        return carry

    lax.fori_loop(0, n_groups, finish_group, 0)

    acc = part[o].astype(jnp.float32)
    for d in range(1, n_ao):
        acc = acc + recv[d - 1].astype(jnp.float32)
    total[...] = acc
    for i in range(width):
        mine[i] = total[:, i, :].astype(jnp.bfloat16)

    band_of = o // ratio
    place = pl.ds(pl.multiple_of(lax.rem(o, ratio) * width, width), width)
    right_copies = []
    for d in range(1, n_aux):
        copy = pltpu.make_async_remote_copy(
            src_ref=mine, dst_ref=right.at[a],
            send_sem=r_send.at[d - 1], recv_sem=r_recv.at[d - 1],
            device_id=(lax.rem(a + d, n_aux), o), device_id_type=MESH,
        )
        right_copies.append(copy)

    def left_copy(d):
        return pltpu.make_async_remote_copy(
            src_ref=mine, dst_ref=left.at[a, place],
            send_sem=l_send.at[d], recv_sem=l_recv.at[a, lax.rem(o, ratio)],
            device_id=(band_of, lax.rem(o + d, n_ao)), device_id_type=MESH,
        )

    home = band_of == a
    for d in range(1, n_ao):
        left_copy(d).start()
    for copy in right_copies:
        copy.start()

    @pl.when(jnp.logical_not(home))
    def _():
        left_copy(0).start()

    own_right = pltpu.make_async_copy(mine, right.at[a], own_sem.at[0])
    own_left = pltpu.make_async_copy(mine, left.at[a, place], own_sem.at[1])
    own_right.start()

    @pl.when(home)
    def _():
        own_left.start()
        own_left.wait()

    own_right.wait()
    for d in range(1, n_ao):
        left_copy(d).wait_send()

    @pl.when(jnp.logical_not(home))
    def _():
        left_copy(0).wait_send()

    for copy in right_copies:
        copy.wait()
    for source in range(n_aux):
        for q in range(ratio):
            @pl.when(jnp.logical_not(jnp.logical_and(source == a, a * ratio + q == o)))
            def _():
                pltpu.make_async_remote_copy(
                    src_ref=mine, dst_ref=left.at[source, pl.ds(q * width, width)],
                    send_sem=l_send.at[0], recv_sem=l_recv.at[source, q],
                    device_id=(band_of, lax.rem(o + 1, n_ao)), device_id_type=MESH,
                ).wait_recv()


def integrals_kernel(left, right, out, wide):
    n_aux, width, nvec, active = right.shape

    @pl.when(pl.program_id(0) == 0)
    def _():
        for source in range(n_aux):
            for i in range(width):
                wide[pl.ds(source * nvec, nvec), pl.ds(i * active, active)] = right[source, i]

    tall = jnp.concatenate(
        [
            jnp.concatenate([left[s, k] for s in range(n_aux)], axis=0)
            for k in range(left.shape[1])
        ],
        axis=1,
    )
    out[...] = lax.dot_general(
        tall, wide[...], (((0,), (0,)), ((), ())), preferred_element_type=jnp.float32
    )


def on_device(n_aux, n_ao, cholesky, coeffs):
    nvec, rows, basis = cholesky.shape
    active = coeffs.shape[1]
    width, band = active // n_ao, active // n_aux
    slab_bytes = rows * basis * 2
    depth = max(2, min(nvec, (36 << 20) // slab_bytes))
    group = max(1, nvec // 4)
    n_groups = nvec // group
    dma = pltpu.SemaphoreType.DMA
    vmem = pl.BlockSpec(memory_space=pltpu.VMEM)
    bf16 = jnp.bfloat16
    left, right = pl.pallas_call(
        functools.partial(pairs_kernel, n_aux, n_ao, depth, group),
        out_shape=(
            jax.ShapeDtypeStruct((n_aux, band, nvec, active), bf16),
            jax.ShapeDtypeStruct((n_aux, width, nvec, active), bf16),
        ),
        in_specs=[pl.BlockSpec(memory_space=pl.ANY), vmem],
        out_specs=(vmem, vmem),
        scratch_shapes=[
            pltpu.VMEM((basis, active), bf16),
            pltpu.VMEM((depth, rows, basis), bf16),
            pltpu.VMEM((n_ao, nvec, width, active), bf16),
            pltpu.VMEM((n_ao - 1, nvec, width, active), bf16),
            pltpu.VMEM((nvec, width, active), jnp.float32),
            pltpu.VMEM((width, nvec, active), bf16),
            dma((depth,)),
            dma((n_ao - 1,)),
            dma((n_ao - 1,)),
            dma((n_groups, n_ao - 1)),
            dma((n_groups, n_ao - 1)),
            dma((n_aux - 1,)),
            dma((n_aux - 1,)),
            dma((n_ao,)),
            dma((n_aux, n_ao // n_aux)),
            dma((2,)),
        ],
        compiler_params=pltpu.CompilerParams(
            has_side_effects=True, vmem_limit_bytes=56 << 20
        ),
    )(cholesky, coeffs)
    per_step = 2
    return pl.pallas_call(
        integrals_kernel,
        grid=(band // per_step,),
        out_shape=jax.ShapeDtypeStruct((band * active, width * active), jnp.float32),
        in_specs=[
            pl.BlockSpec((n_aux, per_step, nvec, active), lambda k: (0, k, 0, 0)),
            pl.BlockSpec((n_aux, width, nvec, active), lambda k: (0, 0, 0, 0)),
        ],
        out_specs=pl.BlockSpec((per_step * active, width * active), lambda k: (k, 0)),
        scratch_shapes=[pltpu.VMEM((n_aux * nvec, width * active), bf16)],
    )(left, right)


def solution(mesh):
    return jax.shard_map(
        functools.partial(on_device, mesh.shape["aux"], mesh.shape["ao"]),
        mesh=mesh,
        in_specs=(P("aux", "ao", None), P("ao", None)),
        out_specs=P("aux", "ao"),
        check_vma=False,
    )
```

profile of v0, /device:TPU:14, one launch (start us, length us, event | category | flops | bytes accessed | tf_op | source)
XLA Modules:
  0.0 89.9 jit_solution(7158098261617024124)
XLA Ops:
  0.0 73.9 %shard_map.28 = (bf16[4,32,16,128]{3,2,1,0:T(8,128)(2,1)}, bf16[4,16,16,128]{3,2,1,0:T(8,128)(2,1)}) custom-call(bf16[16,512,4096]{2,1,0:T(8,128)(2,1)} %chol.1, bf16[512,128]{1,0:T(8,128)(2,1)} %c_ref.1), custom_call_target="tpu_custom_call" | custom-call | tf_op jit(solution)/shard_map/pallas_call | solution.py:189
  73.9 16.0 %shard_map.29 = f32[4096,2048]{1,0:T(8,128)} custom-call(bf16[4,32,16,128]{3,2,1,0:T(8,128)(2,1)} %get-tuple-element.7.left, bf16[4,16,16,128]{3,2,1,0:T(8,128)(2,1)} %get-tuple-element.8.right), custom_call_target="tpu_custom_call" | custom-call | tf_op jit(solution)/shard_map/pallas_call | solution.py:220
where the time goes:
time: 90.6 us; the launch traced here: 89.9 us
  Pallas kernels  89.9 us (99%)
    pallas_call x1, Pallas kernels, on_device(): pl.pallas_call(functools.partial(pairs_kernel, n_aux, n_ao, depth, group)...  73.9 us
    pallas_call x1, Pallas kernels, on_device(): pl.pallas_call(integrals_kernel, grid=(band // per_step,), out_shape=jax....  16 us

commit v1 on v0

v1 whole, which is shorter than its diff:
```python
import functools

import jax
import jax.numpy as jnp
from jax import lax
from jax.experimental import pallas as pl
from jax.experimental.pallas import tpu as pltpu
from jax.sharding import PartitionSpec as P

MESH = pl.DeviceIdType.MESH
F32 = jnp.float32
BF16 = jnp.bfloat16


def dot(a, b):
    return jnp.dot(a, b, preferred_element_type=F32)


def pairs_kernel(
    n_aux, n_ao, n_groups,
    chol, c_ref, left, right,
    slabs, basis, ct, ct_lo, ct_hi, u, part, recv1, part2, recv2, mine,
    slab_sem, c_send, c_recv, f_send, f_recv,
    a1_send, a1_recv, a2_send, a2_recv, r_send, r_recv, l_send, l_recv, y_send, y_recv,
):
    a = lax.axis_index("aux")
    o = lax.axis_index("ao")
    nvec, rows, _ = chol.shape
    active = c_ref.shape[1]
    width = active // n_ao
    reach = n_ao // 2
    nz = n_ao // 2
    half = rows // 2
    fine = half % 128 == 0
    quarter = rows // n_aux
    gv = nvec // n_groups
    y = lax.rem(o, 2)
    z = o // 2
    partner = o + 1 - 2 * y
    ratio = n_ao // n_aux
    hr = ratio // 2
    band_of = o // ratio
    qh = lax.rem(o, ratio) // 2
    home = band_of == a

    def share_copy(d):
        mine_rows = pl.ds(pl.multiple_of(a * quarter, quarter), quarter)
        there = pl.ds(pl.multiple_of(d * rows + a * quarter, quarter), quarter)
        return pltpu.make_async_remote_copy(
            src_ref=c_ref.at[mine_rows], dst_ref=basis.at[there],
            send_sem=c_send.at[d - 1], recv_sem=c_recv.at[d - 1],
            device_id=(a, lax.rem(o + n_ao - d, n_ao)), device_id_type=MESH,
        )

    def forward_copy(d, e):
        there = pl.ds(pl.multiple_of(d * rows + a * quarter, quarter), quarter)
        return pltpu.make_async_remote_copy(
            src_ref=basis.at[there], dst_ref=basis.at[there],
            send_sem=f_send.at[d - 1, e - 1], recv_sem=f_recv.at[d - 1, e - 1],
            device_id=(lax.rem(a + e, n_aux), o), device_id_type=MESH,
        )

    for d in range(1, reach + 1):
        share_copy(d).start()

    deep = (reach + 1) * rows

    def start_vector(v, carry):
        for first in range(n_ao):
            @pl.when(o == first)
            def _():
                run = min(reach + 1, n_ao - first) * rows
                pltpu.make_async_copy(
                    chol.at[v, :, pl.ds(first * rows, run)],
                    slabs.at[v, :, pl.ds(0, run)],
                    slab_sem.at[v],
                ).start()
                if run < deep:
                    pltpu.make_async_copy(
                        chol.at[v, :, pl.ds(0, deep - run)],
                        slabs.at[v, :, pl.ds(run, deep - run)],
                        slab_sem.at[v],
                    ).start()
        return carry

    lax.fori_loop(0, nvec, start_vector, 0)

    basis[pl.ds(0, rows), :] = c_ref[...]
    c_t = c_ref[...].astype(F32).T
    first = lax.broadcasted_iota(jnp.int32, c_t.shape, 1) < (half if fine else 0)
    ct[...] = c_t.astype(BF16)
    ct_lo[...] = jnp.where(first, c_t, 0.5 * c_t).astype(BF16)
    ct_hi[...] = jnp.where(first, 0.5 * c_t, c_t).astype(BF16)

    def contract_rows(v, carry):
        pltpu.make_async_copy(
            chol.at[v, :, pl.ds(0, deep)], slabs.at[v], slab_sem.at[v]
        ).wait()
        out = pl.ds(pl.multiple_of(v * active, active), active)
        if not fine:
            for d in range(reach + 1):
                block = pl.ds(d * rows, rows)
                lhs = ct_lo if d in (0, reach) else ct
                u[out, block] = dot(lhs[...], slabs[v, :, block]).astype(BF16)
            return carry
        lo, hi = pl.ds(0, half), pl.ds(half, half)

        def put(b, value):
            u[out, pl.ds(b * half, half)] = value.astype(BF16)

        put(0, dot(ct_hi[:, lo], slabs[v, lo, pl.ds(0, half)]))
        put(1, dot(ct_lo[...], slabs[v, :, pl.ds(half, half)]))
        for b in range(2, n_ao):
            put(b, dot(ct[...], slabs[v, :, pl.ds(b * half, half)]))
        put(n_ao, dot(ct_hi[...], slabs[v, :, pl.ds(n_ao * half, half)]))
        put(n_ao + 1, dot(ct_lo[:, hi], slabs[v, hi, pl.ds((n_ao + 1) * half, half)]))
        return carry

    def rows_of_group(g):
        lax.fori_loop(g * gv, (g + 1) * gv, contract_rows, 0)

    def a1_copy(g):
        return pltpu.make_async_remote_copy(
            src_ref=part.at[g, 1 - y], dst_ref=recv1.at[g],
            send_sem=a1_send.at[g], recv_sem=a1_recv.at[g],
            device_id=(a, partner), device_id_type=MESH,
        )

    def a2_copy(g, d):
        to = lax.rem(z + d, nz)
        return pltpu.make_async_remote_copy(
            src_ref=part2.at[g, to], dst_ref=recv2.at[g, d - 1],
            send_sem=a2_send.at[g, d - 1], recv_sem=a2_recv.at[g, d - 1],
            device_id=(a, 2 * to + y), device_id_type=MESH,
        )

    def pairs_of_group(g):
        tall = gv * active // 2 if gv % 2 == 0 else gv * active
        x = [dot(u[pl.ds(g * gv * active + r, tall), :], basis[...]) for r in range(0, gv * active, tall)]
        for v in range(gv):
            r = v * active
            one = x[r // tall][r % tall : r % tall + active]
            both = (one + one.T).astype(BF16)
            for q in range(n_ao):
                part[g, q % 2, q // 2, v] = both[q * width : (q + 1) * width]
        a1_copy(g).start()

    def second_level(g):
        a1_copy(g).wait()
        part2[g] = (part[g, y].astype(F32) + recv1[g].astype(F32)).astype(BF16)
        for d in range(1, nz):
            a2_copy(g, d).start()

    def right_copy(g, e):
        return pltpu.make_async_remote_copy(
            src_ref=mine.at[g], dst_ref=right.at[g, a],
            send_sem=r_send.at[g, e - 1], recv_sem=r_recv.at[g, e - 1],
            device_id=(lax.rem(a + e, n_aux), o), device_id_type=MESH,
        )

    def left_copy(g, d):
        to = lax.rem(z + d, nz)
        return pltpu.make_async_remote_copy(
            src_ref=mine.at[g], dst_ref=left.at[g, y, qh, a],
            send_sem=l_send.at[g, d], recv_sem=l_recv.at[g, qh, a],
            device_id=(band_of, 2 * to + y), device_id_type=MESH,
        )

    def y_copy(g):
        return pltpu.make_async_remote_copy(
            src_ref=left.at[g, y], dst_ref=left.at[g, y],
            send_sem=y_send.at[g], recv_sem=y_recv.at[g],
            device_id=(a, partner), device_id_type=MESH,
        )

    def finish_sums(g):
        for d in range(1, nz):
            a2_copy(g, d).wait()
        acc = part2[g, z].astype(F32)
        for d in range(1, nz):
            acc = acc + recv2[g, d - 1].astype(F32)
        done = acc.astype(BF16)
        mine[g] = done
        for d in range(1, nz):
            left_copy(g, d).start()

        @pl.when(jnp.logical_not(home))
        def _():
            left_copy(g, 0).start()

        for e in range(1, n_aux):
            right_copy(g, e).start()
        right[g, a] = done

        @pl.when(home)
        def _():
            left[g, y, qh, a] = done

    def pass_on(g):
        for s in range(n_aux):
            for q in range(hr):
                @pl.when(jnp.logical_not(jnp.logical_and(s == a, a * ratio + 2 * q + y == o)))
                def _():
                    pltpu.make_async_remote_copy(
                        src_ref=mine.at[g], dst_ref=left.at[g, y, q, s],
                        send_sem=l_send.at[g, 0], recv_sem=l_recv.at[g, q, s],
                        device_id=(band_of, lax.rem(o + 1, n_ao)), device_id_type=MESH,
                    ).wait_recv()
        y_copy(g).start()

    def last_waits(g):
        for d in range(1, nz):
            left_copy(g, d).wait_send()

        @pl.when(jnp.logical_not(home))
        def _():
            left_copy(g, 0).wait_send()

        for e in range(1, n_aux):
            right_copy(g, e).wait()
        y_copy(g).wait()

    first_groups = max(1, n_groups // 2)
    rows_of_group(0)
    for d in range(1, reach + 1):
        share_copy(d).wait()
        for e in range(1, n_aux):
            forward_copy(d, e).start()
    for g in range(1, first_groups):
        rows_of_group(g)
    for d in range(1, reach + 1):
        for e in range(1, n_aux):
            forward_copy(d, e).wait()
    ready = first_groups
    for step in range(n_groups + 4):
        if step < n_groups:
            if step >= ready:
                rows_of_group(step)
            pairs_of_group(step)
        if 0 <= step - 1 < n_groups:
            second_level(step - 1)
        if 0 <= step - 2 < n_groups:
            finish_sums(step - 2)
        if 0 <= step - 3 < n_groups:
            pass_on(step - 3)
    for g in range(n_groups):
        last_waits(g)


def integrals_kernel(left, right, out, wide, left_f, right_f):
    n_groups, parities, hr, n_aux, gv, width, active = left.shape
    nvec = n_groups * n_aux * gv
    per_step = out.shape[0] // active

    @pl.when(pl.program_id(0) == 0)
    def _():
        right_f[...] = right[...].reshape(nvec, width, active).astype(F32)
        for i in range(width):
            wide[:, pl.ds(i * active, active)] = right_f[:, i, :].astype(BF16)
        for q in range(parities * hr):
            value = left[:, q % 2, q // 2].reshape(nvec, width, active).astype(F32)
            left_f[q] = value

    k = pl.program_id(0) * per_step
    q, i = k // width, lax.rem(k, width)
    tall = jnp.concatenate(
        [left_f[q, :, i + s, :].astype(BF16) for s in range(per_step)], axis=1
    )
    out[...] = lax.dot_general(
        tall, wide[...], (((0,), (0,)), ((), ())), preferred_element_type=F32
    )


def on_device(n_aux, n_ao, cholesky, coeffs):
    nvec, rows, basis = cholesky.shape
    active = coeffs.shape[1]
    width, band = active // n_ao, active // n_aux
    ratio = n_ao // n_aux
    nz = n_ao // 2
    reach = n_ao // 2
    n_groups = 4 if nvec % 4 == 0 else 1
    gv = nvec // n_groups
    deep = (reach + 1) * rows
    dma = pltpu.SemaphoreType.DMA
    vmem = pl.BlockSpec(memory_space=pltpu.VMEM)
    left_shape = (n_groups, 2, ratio // 2, n_aux, gv, width, active)
    right_shape = (n_groups, n_aux, gv, width, active)
    left, right = pl.pallas_call(
        functools.partial(pairs_kernel, n_aux, n_ao, n_groups),
        out_shape=(
            jax.ShapeDtypeStruct(left_shape, BF16),
            jax.ShapeDtypeStruct(right_shape, BF16),
        ),
        in_specs=[pl.BlockSpec(memory_space=pl.ANY), vmem],
        out_specs=(vmem, vmem),
        scratch_shapes=[
            pltpu.VMEM((nvec, rows, deep), BF16),
            pltpu.VMEM((deep, active), BF16),
            pltpu.VMEM((active, rows), BF16),
            pltpu.VMEM((active, rows), BF16),
            pltpu.VMEM((active, rows), BF16),
            pltpu.VMEM((nvec * active, deep), BF16),
            pltpu.VMEM((n_groups, 2, nz, gv, width, active), BF16),
            pltpu.VMEM((n_groups, nz, gv, width, active), BF16),
            pltpu.VMEM((n_groups, nz, gv, width, active), BF16),
            pltpu.VMEM((n_groups, nz - 1, gv, width, active), BF16),
            pltpu.VMEM((n_groups, gv, width, active), BF16),
            dma((nvec,)),
            dma((reach,)),
            dma((reach,)),
            dma((reach, n_aux - 1)),
            dma((reach, n_aux - 1)),
            dma((n_groups,)),
            dma((n_groups,)),
            dma((n_groups, nz - 1)),
            dma((n_groups, nz - 1)),
            dma((n_groups, n_aux - 1)),
            dma((n_groups, n_aux - 1)),
            dma((n_groups, nz)),
            dma((n_groups, ratio // 2, n_aux)),
            dma((n_groups,)),
            dma((n_groups,)),
        ],
        compiler_params=pltpu.CompilerParams(
            has_side_effects=True, vmem_limit_bytes=62 << 20
        ),
    )(cholesky, coeffs)
    per_step = 4
    whole = lambda *shape: pl.BlockSpec(shape, lambda k: (0,) * len(shape))
    return pl.pallas_call(
        integrals_kernel,
        grid=(band // per_step,),
        out_shape=jax.ShapeDtypeStruct((band * active, width * active), F32),
        in_specs=[whole(*left_shape), whole(*right_shape)],
        out_specs=pl.BlockSpec((per_step * active, width * active), lambda k: (k, 0)),
        scratch_shapes=[
            pltpu.VMEM((n_aux * nvec, width * active), BF16),
            pltpu.VMEM((ratio, n_aux * nvec, width, active), F32),
            pltpu.VMEM((n_aux * nvec, width, active), F32),
        ],
    )(left, right)


def solution(mesh):
    return jax.shard_map(
        functools.partial(on_device, mesh.shape["aux"], mesh.shape["ao"]),
        mesh=mesh,
        in_specs=(P("aux", "ao", None), P("ao", None)),
        out_specs=P("aux", "ao"),
        check_vma=False,
    )
```

time: 90.6 us -> 63.2 us (0.70)
  the two profiles are of different devices: /device:TPU:14 before, /device:TPU:3 now
where the time goes in v1:
time: 63.2 us; the launch traced here: 63.1 us
  Pallas kernels  63.1 us (100%)
    pallas_call x1, Pallas kernels, on_device(): pl.pallas_call(functools.partial(pairs_kernel, n_aux, n_ao, n_groups), ou...  48.8 us
    pallas_call x1, Pallas kernels, on_device(): pl.pallas_call(integrals_kernel, grid=(band // per_step,), out_shape=jax....  14.3 us

profile of v1, /device:TPU:3, one launch (start us, length us, event | category | flops | bytes accessed | tf_op | source)
XLA Modules:
  0.0 63.1 jit_solution(11215075567306628805)
XLA Ops:
  0.0 48.8 %shard_map.28 = (bf16[4,2,1,4,4,16,128]{6,5,4,3,2,1,0:T(8,128)(2,1)}, bf16[4,4,4,16,128]{4,3,2,1,0:T(8,128)(2,1)}) custom-call(bf16[16,512,4096]{2,1,0:T(8,128)(2,1)} %chol.1, bf16[512,128]{1,0:T(8,128)(2,1)} %c_ref.1), custom_call_target="tpu_custom_call" | custom-call | tf_op jit(solution)/shard_map/pallas_call | solution.py:288
  48.8 14.3 %shard_map.29 = f32[4096,2048]{1,0:T(8,128)} custom-call(bf16[4,2,1,4,4,16,128]{6,5,4,3,2,1,0:T(8,128)(2,1)} %get-tuple-element.7.left, bf16[4,4,4,16,128]{4,3,2,1,0:T(8,128)(2,1)} %get-tuple-element.8.right), custom_call_target="tpu_custom_call" | custom-call | tf_op jit(solution)/shard_map/pallas_call | solution.py:330
